TPU v7x, 32 devices: a whole 2x2x4 slice. The times are simulated.
32 devices in a mesh: grp: 2 (over y), row: 4 (over x, core), col: 4 (over z).
Axes of the slice: x: 2, y: 2, z: 4, core: 2. Of those that a mesh axis runs over, the one named last changes fastest.
Arguments:
- perturbation: bfloat16 [4, 12000, 12000], P('grp', 'row', 'col'), parts along dimension 0, may hold values from -96 to 96
- occ_coeffs: bfloat16 [12000, 2000], P('row', 'col'), may hold values from -0.0546875 to 0.0546875
- vir_coeffs: bfloat16 [12000, 512], P('col', 'row'), may hold values from -0.0546875 to 0.0546875
- occ_energies: float32 [2000], replicated, may hold values from -1 to -0.1
- vir_energies: float32 [512], replicated, may hold values from 0.1 to 1.5
Outputs:
- density_response: bfloat16 [4, 12000, 12000], P('grp', 'row', 'col'), parts along dimension 0
There are 2 independent parts, one for each index of `grp`. A program takes and returns all parts, laid end to end along the dimension named above; an argument that names none is the same for every part. Nothing has to cross between parts.
All inputs are finite; a program needn't handle non-finite values.
Results may differ from a plain program's by a relative error of at most 0.0098.
Values may be sent and summed in bfloat16 or wider, within the bound.
A program may use at most 192 MiB of HBM per device.

v0:
```python
import jax
import jax.numpy as jnp
from jax import lax
from jax.sharding import PartitionSpec as P


def per_device(perturbation, occ_coeffs, vir_coeffs, occ_energies, vir_energies):
    occ_rows = lax.all_gather(occ_coeffs, "col", axis=1, tiled=True)
    vir_rows = lax.all_gather(vir_coeffs, "row", axis=1, tiled=True)
    image = jnp.einsum("pij,jv->piv", perturbation, vir_rows, preferred_element_type=jnp.float32)
    image = lax.psum(image, "col")
    partial_value = jnp.einsum(
        "io,piv->pov", occ_rows.astype(jnp.float32), image, precision=lax.Precision.HIGHEST
    )
    coupling = lax.psum(partial_value, "row")
    gaps = occ_energies[:, None] - vir_energies[None, :]
    response = (coupling / gaps[None, :, :]).astype(jnp.bfloat16)
    mixed = jnp.einsum(
        "io,pov->piv", occ_rows, response, preferred_element_type=jnp.float32
    ).astype(jnp.bfloat16)
    return jnp.einsum("piv,jv->pij", mixed, vir_rows, preferred_element_type=jnp.float32).astype(
        jnp.bfloat16
    )


def solution(mesh):
    placed = (P("grp", "row", "col"), P("row", "col"), P("col", "row"), P(), P())
    return jax.shard_map(
        per_device, mesh=mesh, in_specs=placed, out_specs=P("grp", "row", "col"), check_vma=False
    )
```

profile of v0, /device:TPU:0, one launch (start us, length us, event | category | flops | bytes accessed | tf_op | source)
XLA Modules:
  0.0 920.3 jit_solution(8147711302796807755)
XLA Ops:
  6.5 0.0 all-gather.4.cloned.1.call-start
  6.5 0.7 all-gather.4.cloned.1.call-update
  7.3 0.0 all-gather.6.cloned.1.call-start
  7.3 0.7 all-gather.6.cloned.1.call-update
  8.0 0.0 all-reduce.3.cloned.1.call-start
  8.1 32.1 %all-gather.4.cloned.1.call-done = bf16[3000,512]{1,0:T(8,128)(2,1)} async-done(((bf16[3000,128]{1,0:T(8,128)(2,1)}), bf16[3000,512]{1,0:T(8,128)(2,1)}) %all-gather.4.cloned.1.call-update) | async-done | bytes 3072016 | tf_op jit(solution)/shard_map/all_gather | solution.py:9
  40.1 26.8 %fusion.6 = f32[2,3000,512]{2,1,0:T(8,128)} fusion(bf16[2,3000,3000]{2,1,0:T(8,128)(2,1)} %param.5, bf16[3000,512]{1,0:T(8,128)(2,1)} %all-gather.4.cloned.1.call-done), kind=kOutput, calls=%fused_computation.9 | convolution fusion | flops 18432000000 | bytes 51360000 | tf_op jit(solution)/shard_map/pij,jv->piv/dot_general | solution.py:10
  66.9 0.0 all-reduce.3.cloned.1.call-update
  66.9 0.0 all-reduce.5.cloned.1.call-start
  67.0 188.1 %all-gather.6.cloned.1.call-done = bf16[4,500,3000]{1,2,0:T(8,128)(2,1)} async-done(((bf16[1,500,3000]{1,2,0:T(8,128)(2,1)}), bf16[4,500,3000]{1,2,0:T(8,128)(2,1)}) %all-gather.6.cloned.1.call-update) | async-done | bytes 12000016 | tf_op jit(solution)/shard_map/all_gather | solution.py:8
  255.1 16.1 %copy.7 = bf16[4,500,3000]{2,1,0:T(8,128)(2,1)} copy(bf16[4,500,3000]{1,2,0:T(8,128)(2,1)} %all-gather.6.cloned.1.call-done) | data formatting | bytes 24000000 | tf_op jit(solution)/shard_map/all_gather | solution.py:8
  271.2 16.2 %reshape.30 = bf16[2000,3000,1]{1,0,2:T(8,128)(2,1)} reshape(bf16[4,500,3000]{2,1,0:T(8,128)(2,1)} %copy.7) | data formatting | bytes 24000000
  287.4 385.4 %all-reduce.3.cloned.1.call-done = f32[2,3000,512]{2,1,0:T(8,128)} async-done(((f32[2,3000,512]{2,1,0:T(8,128)}), f32[2,3000,512]{2,1,0:T(8,128)}) %all-reduce.3.cloned.1.call-update) | async-done | bytes 12288016 | tf_op jit(solution)/shard_map/psum | solution.py:11
  672.7 44.9 %convolution_bitcast_fusion = f32[2,2000,512]{2,1,0:T(8,128)} fusion(f32[2,3000,512]{2,1,0:T(8,128)} %all-reduce.3.cloned.1.call-done, bf16[2000,3000,1]{1,0,2:T(8,128)(2,1)} %reshape.30), kind=kOutput, calls=%fused_computation.6 | convolution fusion | flops 73728000000 | bytes 32480000 | tf_op jit(solution)/shard_map/io,piv->pov/dot_general | solution.py:12
  717.7 0.0 copy-start
  717.7 0.0 all-reduce.5.cloned.1.call-update
  717.7 0.7 copy-done
  718.4 0.0 copy-done.1
  718.4 2.3 broadcast_subtract_fusion
  720.7 17.0 %reshape.28 = bf16[2000,3000]{1,0:T(8,128)(2,1)} reshape(bf16[4,500,3000]{2,1,0:T(8,128)(2,1)} %copy.7) | data formatting | bytes 24000000
  737.7 128.8 %all-reduce.5.cloned.1.call-done = f32[2,2000,512]{2,1,0:T(8,128)} async-done(((f32[2,2000,512]{2,1,0:T(8,128)}), f32[2,2000,512]{2,1,0:T(8,128)}) %all-reduce.5.cloned.1.call-update) | async-done | bytes 8192016 | tf_op jit(solution)/shard_map/psum | solution.py:15
  866.5 20.9 %fusion = bf16[2,512,3000]{1,2,0:T(8,128)(2,1)} fusion(bf16[2000,3000]{1,0:T(8,128)(2,1)} %reshape.28, f32[2,2000,512]{2,1,0:T(8,128)} %all-reduce.5.cloned.1.call-done, f32[2000,512]{1,0:T(8,128)} %broadcast_subtract_fusion), kind=kOutput, calls=%fused_computation.1 | convolution fusion | flops 12292096000 | bytes 30432000 | tf_op jit(solution)/shard_map/io,pov->piv/dot_general | solution.py:18
  887.3 0.0 copy-done.2
  887.3 26.4 %convolution_convert_fusion = bf16[2,3000,3000]{2,1,0:T(8,128)(2,1)} fusion(bf16[2,512,3000]{1,2,0:T(8,128)(2,1)} %fusion, bf16[3000,512]{1,0:T(8,128)(2,1)S(1)} %copy-done.2), kind=kOutput, calls=%fused_computation | convolution fusion | flops 18449999872 | bytes 45216000 | tf_op jit(solution)/shard_map/piv,jv->pij/dot_general | solution.py:21
  (2 shorter events, 0.0 us)
Async XLA Ops:
  6.5 33.6 %all-gather.4.cloned.1.call-start = ((), (), s32[]{:S(2)}) async-start(), calls=%async_computation | async-start | bytes 3840000 | tf_op jit(solution)/shard_map/all_gather | solution.py:9
  7.3 247.8 %all-gather.6.cloned.1.call-start = ((), (), s32[]{:S(2)}) async-start(), calls=%async_computation.3 | async-start | bytes 15360000 | tf_op jit(solution)/shard_map/all_gather | solution.py:8
  8.0 664.7 %all-reduce.3.cloned.1.call-start = ((), (), s32[]{:S(2)}) async-start(), calls=%async_computation.1 | async-start | bytes 24576000 | tf_op jit(solution)/shard_map/psum | solution.py:11
  66.9 799.5 %all-reduce.5.cloned.1.call-start = ((), (), s32[]{:S(2)}) async-start(), calls=%async_computation.2 | async-start | bytes 16384000 | tf_op jit(solution)/shard_map/psum | solution.py:15
  717.7 0.7 copy-start
  717.7 0.7 copy-start.1
  737.7 149.7 %copy-start.2 = (bf16[3000,512]{1,0:T(8,128)(2,1)S(1)}, bf16[3000,512]{1,0:T(8,128)(2,1)}, u32[]{:S(2)}) copy-start(bf16[3000,512]{1,0:T(8,128)(2,1)} %all-gather.4.cloned.1.call-done) | copy-start | bytes 9216004
Sparse Core Ops, SparseCore 0:
  8.9 31.1 all-gather.3
  41.7 213.3 all-gather.5
  257.6 415.1 all-reduce.2
  717.8 148.6 all-reduce.4
where the time goes:
time: 921 us; the launch traced here: 920 us
  waiting for transfers between devices  736 us (80%)
  matrix products  119 us (13%)
  local copies, waits for them, and re-layouts  50 us (5%)
  between operations  13.1 us (1%)
    psum x1, waiting for transfers between devices, per_device(): image = lax.psum(image, 'col')  385 us
    all_gather x1, waiting for transfers between devices, per_device(): occ_rows = lax.all_gather(occ_coeffs, 'col', axis=1, tiled=True)  188 us
    psum x1, waiting for transfers between devices, per_device(): coupling = lax.psum(partial_value, 'row')  129 us
    dot_general x1, matrix products, per_device(): jnp.einsum('io,piv->pov', occ_rows.astype(jnp.float32), image, precision=...  44.9 us
    unnamed x8, local copies, waits for them, and re-layouts  33.9 us
    all_gather x1, waiting for transfers between devices, per_device(): vir_rows = lax.all_gather(vir_coeffs, 'row', axis=1, tiled=True)  32.1 us
    dot_general x1, matrix products, per_device(): jnp.einsum('pij,jv->piv', perturbation, vir_rows, preferred_element_type=...  26.8 us
    dot_general x1, matrix products, per_device(): jnp.einsum('piv,jv->pij', mixed, vir_rows, preferred_element_type=jnp.flo...  26.4 us
  transfers between devices with their start and end apart: 4, of which 4 were waited for; matrix products, arithmetic and copies ran while one was open for 9% of the time, Pallas kernels for 0%

commit v1 on v0

--- a/solution.py
+++ b/solution.py
@@ -8,7 +8,9 @@
     occ_rows = lax.all_gather(occ_coeffs, "col", axis=1, tiled=True)
     vir_rows = lax.all_gather(vir_coeffs, "row", axis=1, tiled=True)
     image = jnp.einsum("pij,jv->piv", perturbation, vir_rows, preferred_element_type=jnp.float32)
-    image = lax.psum(image, "col")
+    image = image
+    for hop in (1, 2):
+        image = image + lax.ppermute(image, "col", [(dev, dev ^ hop) for dev in range(4)])
     partial_value = jnp.einsum(
         "io,piv->pov", occ_rows.astype(jnp.float32), image, precision=lax.Precision.HIGHEST
     )

time: 921 us -> 1330 us (1.44)
  waiting for transfers between devices: 736 us -> 1120 us
  other arithmetic: 2.29 us -> 16.4 us
    ppermute x0 -> x2, waiting for transfers between devices: none -> 957 us  [per_device(): lax.ppermute(image, 'col', [(dev, dev ^ hop) for dev in range(4)])]
    psum x1 -> x0, waiting for transfers between devices: 385 us -> none  [per_device(): image = lax.psum(image, 'col')]
    all_gather x1, waiting for transfers between devices: 188 us -> 0.01 us  [per_device(): occ_rows = lax.all_gather(occ_coeffs, 'col', axis=1, tiled=True)]
    add x0 -> x1, other arithmetic: none -> 14.1 us  [per_device(): image + lax.ppermute(image, 'col', [(dev, dev ^ hop) for dev in range(4)])]
  transfers between devices with their start and end apart: 4 -> 5, of which waited for: 4 -> 4; matrix products, arithmetic and copies ran while one was open for 9% -> 5% of each run, Pallas kernels for 0% -> 0%
where the time goes in v1:
time: 1330 us
  waiting for transfers between devices  1120 us (84%)
  matrix products  123 us (9%)
  local copies, waits for them, and re-layouts  49.1 us (4%)
  other arithmetic  16.4 us (1%)
  between operations  14.9 us (1%)
    ppermute x2, waiting for transfers between devices, per_device(): lax.ppermute(image, 'col', [(dev, dev ^ hop) for dev in range(4)])  957 us
    psum x1, waiting for transfers between devices, per_device(): coupling = lax.psum(partial_value, 'row')  131 us
    dot_general x1, matrix products, per_device(): jnp.einsum('io,piv->pov', occ_rows.astype(jnp.float32), image, precision=...  49.8 us
    all_gather x1, waiting for transfers between devices, per_device(): vir_rows = lax.all_gather(vir_coeffs, 'row', axis=1, tiled=True)  32.8 us
    unnamed x8, local copies, waits for them, and re-layouts  32.4 us
  transfers between devices with their start and end apart: 5, of which 4 were waited for; matrix products, arithmetic and copies ran while one was open for 5% of the time, Pallas kernels for 0%

profile of v1, /device:TPU:0, one launch (start us, length us, event | category | flops | bytes accessed | tf_op | source)
XLA Modules:
  0.0 1329.4 jit_solution(4852278888481968248)
XLA Ops:
  7.4 0.0 all-gather.4.cloned.1.call-start
  7.4 0.7 all-gather.4.cloned.1.call-update
  8.1 0.0 all-gather.6.cloned.1.call-start
  8.1 32.8 %all-gather.4.cloned.1.call-done = bf16[3000,512]{1,0:T(8,128)(2,1)} async-done(((bf16[3000,128]{1,0:T(8,128)(2,1)}), bf16[3000,512]{1,0:T(8,128)(2,1)}) %all-gather.4.cloned.1.call-update) | async-done | bytes 3072016 | tf_op jit(solution)/shard_map/all_gather | solution.py:9
  40.9 26.1 %fusion.11 = f32[2,3000,512]{2,1,0:T(8,128)} fusion(bf16[2,3000,3000]{2,1,0:T(8,128)(2,1)} %param.5, bf16[3000,512]{1,0:T(8,128)(2,1)} %all-gather.4.cloned.1.call-done), kind=kOutput, calls=%fused_computation.11 | convolution fusion | flops 18432000000 | bytes 51360000 | tf_op jit(solution)/shard_map/pij,jv->piv/dot_general | solution.py:10
  67.0 1.5 collective-permute-start
  68.5 0.0 all-gather.6.cloned.1.call-update
  68.5 0.0 all-reduce.2.cloned.1.call-start
  68.6 462.4 %collective-permute-done = f32[2,3000,512]{2,1,0:T(8,128)} collective-permute-done((f32[2,3000,512]{2,1,0:T(8,128)}, f32[2,3000,512]{2,1,0:T(8,128)}, u32[]{:S(2)}, u32[]{:S(2)}) %collective-permute-start) | collective-permute-done | bytes 12288032 | tf_op jit(solution)/shard_map/ppermute | solution.py:13
  531.0 14.1 %add.8 = f32[2,3000,512]{2,1,0:T(8,128)} add(f32[2,3000,512]{2,1,0:T(8,128)} %fusion.11, f32[2,3000,512]{2,1,0:T(8,128)} %collective-permute-done) | non-fusion elementwise | flops 3072000 | bytes 36864000 | tf_op jit(solution)/shard_map/add | solution.py:13
  545.1 2.4 collective-permute-start.1
  547.5 16.7 %copy.7 = bf16[4,500,3000]{2,1,0:T(8,128)(2,1)} copy(bf16[4,500,3000]{1,2,0:T(8,128)(2,1)} %all-gather.6.cloned.1.call-done) | data formatting | bytes 24000000 | tf_op jit(solution)/shard_map/all_gather | solution.py:8
  564.2 16.2 %reshape.30 = bf16[2000,3000,1]{1,0,2:T(8,128)(2,1)} reshape(bf16[4,500,3000]{2,1,0:T(8,128)(2,1)} %copy.7) | data formatting | bytes 24000000
  580.4 494.6 %collective-permute-done.1 = f32[2,3000,512]{2,1,0:T(8,128)} collective-permute-done((f32[2,3000,512]{2,1,0:T(8,128)}, f32[2,3000,512]{2,1,0:T(8,128)}, u32[]{:S(2)}, u32[]{:S(2)}) %collective-permute-start.1) | collective-permute-done | bytes 12288032 | tf_op jit(solution)/shard_map/ppermute | solution.py:13
  1074.9 49.8 %fusion.6 = f32[2,2000,512]{2,1,0:T(8,128)} fusion(bf16[2000,3000,1]{1,0,2:T(8,128)(2,1)} %reshape.30, f32[2,3000,512]{2,1,0:T(8,128)} %add.8, f32[2,3000,512]{2,1,0:T(8,128)} %collective-permute-done.1), kind=kOutput, calls=%fused_computation.8 | convolution fusion | flops 73731072000 | bytes 44768000 | tf_op jit(solution)/shard_map/io,piv->pov/dot_general | solution.py:14
  1124.7 0.0 all-reduce.2.cloned.1.call-update
  1124.8 0.0 copy-done
  1124.8 0.0 copy-done.1
  1124.8 2.4 broadcast_subtract_fusion
  1127.2 16.2 %reshape.28 = bf16[2000,3000]{1,0:T(8,128)(2,1)} reshape(bf16[4,500,3000]{2,1,0:T(8,128)(2,1)} %copy.7) | data formatting | bytes 24000000
  1143.4 131.2 %all-reduce.2.cloned.1.call-done = f32[2,2000,512]{2,1,0:T(8,128)} async-done(((f32[2,2000,512]{2,1,0:T(8,128)}), f32[2,2000,512]{2,1,0:T(8,128)}) %all-reduce.2.cloned.1.call-update) | async-done | bytes 8192016 | tf_op jit(solution)/shard_map/psum | solution.py:17
  1274.6 20.9 %fusion = bf16[2,512,3000]{1,2,0:T(8,128)(2,1)} fusion(bf16[2000,3000]{1,0:T(8,128)(2,1)} %reshape.28, f32[2,2000,512]{2,1,0:T(8,128)} %all-reduce.2.cloned.1.call-done, f32[2000,512]{1,0:T(8,128)} %broadcast_subtract_fusion), kind=kOutput, calls=%fused_computation.1 | convolution fusion | flops 12292096000 | bytes 30432000 | tf_op jit(solution)/shard_map/io,pov->piv/dot_general | solution.py:20
  1295.5 0.0 copy-done.2
  1295.5 26.4 %convolution_convert_fusion = bf16[2,3000,3000]{2,1,0:T(8,128)(2,1)} fusion(bf16[2,512,3000]{1,2,0:T(8,128)(2,1)} %fusion, bf16[3000,512]{1,0:T(8,128)(2,1)S(1)} %copy-done.2), kind=kOutput, calls=%fused_computation | convolution fusion | flops 18449999872 | bytes 45216000 | tf_op jit(solution)/shard_map/piv,jv->pij/dot_general | solution.py:23
  (4 shorter events, 0.0 us)
Async XLA Ops:
  7.4 33.6 %all-gather.4.cloned.1.call-start = ((), (), s32[]{:S(2)}) async-start(), calls=%async_computation | async-start | bytes 3840000 | tf_op jit(solution)/shard_map/all_gather | solution.py:9
  8.1 539.4 %all-gather.6.cloned.1.call-start = ((), (), s32[]{:S(2)}) async-start(), calls=%async_computation.2 | async-start | bytes 15360000 | tf_op jit(solution)/shard_map/all_gather | solution.py:8
  67.0 464.0 %collective-permute-start = (f32[2,3000,512]{2,1,0:T(8,128)}, f32[2,3000,512]{2,1,0:T(8,128)}, u32[]{:S(2)}, u32[]{:S(2)}) collective-permute-start(f32[2,3000,512]{2,1,0:T(8,128)} %fusion.11), channel_id=1, source_target_pairs={{0,1},{1,0},{2,3},{3,2},{4,5},{5,4},{6,7},{7,6},{8,9},{9,8},{10,11... | collective-permute-start | bytes 36864008 | tf_op jit(solution)/shard_map/ppermute | solution.py:13
  68.5 1206.0 %all-reduce.2.cloned.1.call-start = ((), (), s32[]{:S(2)}) async-start(), calls=%async_computation.1 | async-start | bytes 16384000 | tf_op jit(solution)/shard_map/psum | solution.py:17
  545.1 529.9 %collective-permute-start.1 = (f32[2,3000,512]{2,1,0:T(8,128)}, f32[2,3000,512]{2,1,0:T(8,128)}, u32[]{:S(2)}, u32[]{:S(2)}) collective-permute-start(f32[2,3000,512]{2,1,0:T(8,128)} %add.8), channel_id=1, source_target_pairs={{0,2},{1,3},{2,0},{3,1},{4,6},{5,7},{6,4},{7,5},{8,10},{9,11},{10,... | collective-permute-start | bytes 36864008 | tf_op jit(solution)/shard_map/ppermute | solution.py:13
  580.3 544.4 %copy-start = (f32[2000]{0:T(1024)S(1)}, f32[2000]{0:T(1024)}, u32[]{:S(2)}) copy-start(f32[2000]{0:T(1024)} %param.8) | copy-start | bytes 24004
  580.3 544.4 %copy-start.1 = (f32[512]{0:T(512)S(1)}, f32[512]{0:T(512)}, u32[]{:S(2)}) copy-start(f32[512]{0:T(512)} %param.9) | copy-start | bytes 6148
  1143.4 152.1 %copy-start.2 = (bf16[3000,512]{1,0:T(8,128)(2,1)S(1)}, bf16[3000,512]{1,0:T(8,128)(2,1)}, u32[]{:S(2)}) copy-start(bf16[3000,512]{1,0:T(8,128)(2,1)} %all-gather.4.cloned.1.call-done) | copy-start | bytes 9216004
Sparse Core Ops, SparseCore 0:
  9.7 31.1 all-gather.3
  1124.9 149.6 all-reduce.1
Sparse Core Ops, SparseCore 1:
  68.6 405.1 all-gather.5

commit v2 on v0

--- a/solution.py
+++ b/solution.py
@@ -12,7 +12,9 @@
     partial_value = jnp.einsum(
         "io,piv->pov", occ_rows.astype(jnp.float32), image, precision=lax.Precision.HIGHEST
     )
-    coupling = lax.psum(partial_value, "row")
+    coupling = partial_value
+    for hop in (1, 2):
+        coupling = coupling + lax.ppermute(coupling, "row", [(dev, dev ^ hop) for dev in range(4)])
     gaps = occ_energies[:, None] - vir_energies[None, :]
     response = (coupling / gaps[None, :, :]).astype(jnp.bfloat16)
     mixed = jnp.einsum(

time: 921 us -> 976 us (1.060)
  waiting for transfers between devices: 736 us -> 778 us
    ppermute x0 -> x2, waiting for transfers between devices: none -> 172 us  [per_device(): lax.ppermute(coupling, 'row', [(dev, dev ^ hop) for dev in range(4)])]
    psum x1 -> x0, waiting for transfers between devices: 129 us -> none  [per_device(): coupling = lax.psum(partial_value, 'row')]
  transfers between devices with their start and end apart: 4 -> 5, of which waited for: 4 -> 5; matrix products, arithmetic and copies ran while one was open for 9% -> 8% of each run, Pallas kernels for 0% -> 0%
where the time goes in v2:
time: 976 us; the launch traced here: 975 us
  waiting for transfers between devices  778 us (80%)
  matrix products  122 us (12%)
  local copies, waits for them, and re-layouts  48.5 us (5%)
  between operations  13.1 us (1%)
  other arithmetic  10.9 us (1%)
    psum x1, waiting for transfers between devices, per_device(): image = lax.psum(image, 'col')  385 us
    all_gather x1, waiting for transfers between devices, per_device(): occ_rows = lax.all_gather(occ_coeffs, 'col', axis=1, tiled=True)  188 us
    ppermute x2, waiting for transfers between devices, per_device(): lax.ppermute(coupling, 'row', [(dev, dev ^ hop) for dev in range(4)])  172 us
    dot_general x1, matrix products, per_device(): jnp.einsum('io,piv->pov', occ_rows.astype(jnp.float32), image, precision=...  45.6 us
    unnamed x8, local copies, waits for them, and re-layouts  32.3 us
    all_gather x1, waiting for transfers between devices, per_device(): vir_rows = lax.all_gather(vir_coeffs, 'row', axis=1, tiled=True)  32.1 us
    dot_general x1, matrix products, per_device(): jnp.einsum('pij,jv->piv', perturbation, vir_rows, preferred_element_type=...  26.9 us
    dot_general x1, matrix products, per_device(): jnp.einsum('piv,jv->pij', mixed, vir_rows, preferred_element_type=jnp.flo...  26.4 us
  transfers between devices with their start and end apart: 5, of which 5 were waited for; matrix products, arithmetic and copies ran while one was open for 8% of the time, Pallas kernels for 0%

profile of v2, /device:TPU:0, one launch (start us, length us, event | category | flops | bytes accessed | tf_op | source)
XLA Modules:
  0.0 975.0 jit_solution(6560987757880370045)
XLA Ops:
  6.5 0.0 all-gather.4.cloned.1.call-start
  6.5 0.7 all-gather.4.cloned.1.call-update
  7.3 0.0 all-gather.6.cloned.1.call-start
  7.3 0.7 all-gather.6.cloned.1.call-update
  8.0 0.0 all-reduce.2.cloned.1.call-start
  8.1 32.1 %all-gather.4.cloned.1.call-done = bf16[3000,512]{1,0:T(8,128)(2,1)} async-done(((bf16[3000,128]{1,0:T(8,128)(2,1)}), bf16[3000,512]{1,0:T(8,128)(2,1)}) %all-gather.4.cloned.1.call-update) | async-done | bytes 3072016 | tf_op jit(solution)/shard_map/all_gather | solution.py:9
  40.1 26.9 %fusion.6 = f32[2,3000,512]{2,1,0:T(8,128)} fusion(bf16[2,3000,3000]{2,1,0:T(8,128)(2,1)} %param.5, bf16[3000,512]{1,0:T(8,128)(2,1)} %all-gather.4.cloned.1.call-done), kind=kOutput, calls=%fused_computation.9 | convolution fusion | flops 18432000000 | bytes 51360000 | tf_op jit(solution)/shard_map/pij,jv->piv/dot_general | solution.py:10
  67.0 0.0 all-reduce.2.cloned.1.call-update
  67.1 188.0 %all-gather.6.cloned.1.call-done = bf16[4,500,3000]{1,2,0:T(8,128)(2,1)} async-done(((bf16[1,500,3000]{1,2,0:T(8,128)(2,1)}), bf16[4,500,3000]{1,2,0:T(8,128)(2,1)}) %all-gather.6.cloned.1.call-update) | async-done | bytes 12000016 | tf_op jit(solution)/shard_map/all_gather | solution.py:8
  255.1 16.1 %copy.8 = bf16[4,500,3000]{2,1,0:T(8,128)(2,1)} copy(bf16[4,500,3000]{1,2,0:T(8,128)(2,1)} %all-gather.6.cloned.1.call-done) | data formatting | bytes 24000000 | tf_op jit(solution)/shard_map/all_gather | solution.py:8
  271.2 16.2 %reshape.30 = bf16[2000,3000,1]{1,0,2:T(8,128)(2,1)} reshape(bf16[4,500,3000]{2,1,0:T(8,128)(2,1)} %copy.8) | data formatting | bytes 24000000
  287.4 385.4 %all-reduce.2.cloned.1.call-done = f32[2,3000,512]{2,1,0:T(8,128)} async-done(((f32[2,3000,512]{2,1,0:T(8,128)}), f32[2,3000,512]{2,1,0:T(8,128)}) %all-reduce.2.cloned.1.call-update) | async-done | bytes 12288016 | tf_op jit(solution)/shard_map/psum | solution.py:11
  672.7 45.6 %convolution_bitcast_fusion = f32[2,2000,512]{2,1,0:T(8,128)S(1)} fusion(f32[2,3000,512]{2,1,0:T(8,128)} %all-reduce.2.cloned.1.call-done, bf16[2000,3000,1]{1,0,2:T(8,128)(2,1)} %reshape.30), kind=kOutput, calls=%fused_computation.6 | convolution fusion | flops 73728000000 | bytes 32480000 | tf_op jit(solution)/shard_map/io,piv->pov/dot_general | solution.py:12
  718.3 0.0 copy-start
  718.4 0.0 copy-start.1
  718.4 0.1 collective-permute-start
  718.4 13.0 %collective-permute-done = f32[2,2000,512]{2,1,0:T(8,128)} collective-permute-done((f32[2,2000,512]{2,1,0:T(8,128)S(1)}, f32[2,2000,512]{2,1,0:T(8,128)}, u32[]{:S(2)}, u32[]{:S(2)}) %collective-permute-start) | collective-permute-done | bytes 8192032 | tf_op jit(solution)/shard_map/ppermute | solution.py:17
  731.4 8.5 add.8
  740.0 1.5 collective-permute-start.1
  741.4 2.3 broadcast_subtract_fusion
  743.8 16.2 %reshape.28 = bf16[2000,3000]{1,0:T(8,128)(2,1)} reshape(bf16[4,500,3000]{2,1,0:T(8,128)(2,1)} %copy.8) | data formatting | bytes 24000000
  759.9 158.6 %collective-permute-done.1 = f32[2,2000,512]{2,1,0:T(8,128)} collective-permute-done((f32[2,2000,512]{2,1,0:T(8,128)}, f32[2,2000,512]{2,1,0:T(8,128)}, u32[]{:S(2)}, u32[]{:S(2)}) %collective-permute-start.1) | collective-permute-done | bytes 8192032 | tf_op jit(solution)/shard_map/ppermute | solution.py:17
  918.6 23.4 %fusion = bf16[2,512,3000]{1,2,0:T(8,128)(2,1)} fusion(bf16[2000,3000]{1,0:T(8,128)(2,1)} %reshape.28, f32[2,2000,512]{2,1,0:T(8,128)} %add.8, f32[2,2000,512]{2,1,0:T(8,128)} %collective-permute-done.1, f32[2000,512]{1,0:T(8,128)} %broadcast_subtract_fusion), kind=kOutput, calls=%fused_computation.1 | convolution fusion | flops 12294144000 | bytes 38624000 | tf_op jit(solution)/shard_map/io,pov->piv/dot_general | solution.py:20
  942.0 26.4 %convolution_convert_fusion = bf16[2,3000,3000]{2,1,0:T(8,128)(2,1)} fusion(bf16[2,512,3000]{1,2,0:T(8,128)(2,1)} %fusion, bf16[3000,512]{1,0:T(8,128)(2,1)S(1)} %copy-done.2), kind=kOutput, calls=%fused_computation | convolution fusion | flops 18449999872 | bytes 45216000 | tf_op jit(solution)/shard_map/piv,jv->pij/dot_general | solution.py:23
  (4 shorter events, 0.0 us)
Async XLA Ops:
  6.5 33.6 %all-gather.4.cloned.1.call-start = ((), (), s32[]{:S(2)}) async-start(), calls=%async_computation | async-start | bytes 3840000 | tf_op jit(solution)/shard_map/all_gather | solution.py:9
  7.3 247.8 %all-gather.6.cloned.1.call-start = ((), (), s32[]{:S(2)}) async-start(), calls=%async_computation.2 | async-start | bytes 15360000 | tf_op jit(solution)/shard_map/all_gather | solution.py:8
  8.0 664.7 %all-reduce.2.cloned.1.call-start = ((), (), s32[]{:S(2)}) async-start(), calls=%async_computation.1 | async-start | bytes 24576000 | tf_op jit(solution)/shard_map/psum | solution.py:11
  718.3 23.1 %copy-start = (f32[2000]{0:T(1024)S(1)}, f32[2000]{0:T(1024)}, u32[]{:S(2)}) copy-start(f32[2000]{0:T(1024)} %param.8) | copy-start | bytes 24004
  718.4 23.1 %copy-start.1 = (f32[512]{0:T(512)S(1)}, f32[512]{0:T(512)}, u32[]{:S(2)}) copy-start(f32[512]{0:T(512)} %param.9) | copy-start | bytes 6148
  718.4 13.1 %collective-permute-start = (f32[2,2000,512]{2,1,0:T(8,128)S(1)}, f32[2,2000,512]{2,1,0:T(8,128)}, u32[]{:S(2)}, u32[]{:S(2)}) collective-permute-start(f32[2,2000,512]{2,1,0:T(8,128)S(1)} %convolution_bitcast_fusion), channel_id=1, source_target_pairs={{0,4},{4,0},{8,12},{12,8},{1,5},{5,1},{9,13},{13,9},{2,6},{6,2},{1... | collective-permute-start | bytes 24576008 | tf_op jit(solution)/shard_map/ppermute | solution.py:17
  740.0 178.6 %collective-permute-start.1 = (f32[2,2000,512]{2,1,0:T(8,128)}, f32[2,2000,512]{2,1,0:T(8,128)}, u32[]{:S(2)}, u32[]{:S(2)}) collective-permute-start(f32[2,2000,512]{2,1,0:T(8,128)} %add.8), channel_id=1, source_target_pairs={{0,8},{4,12},{8,0},{12,4},{1,9},{5,13},{9,1},{13,5},{2,10},{6,14},... | collective-permute-start | bytes 24576008 | tf_op jit(solution)/shard_map/ppermute | solution.py:17
  759.9 182.0 %copy-start.2 = (bf16[3000,512]{1,0:T(8,128)(2,1)S(1)}, bf16[3000,512]{1,0:T(8,128)(2,1)}, u32[]{:S(2)}) copy-start(bf16[3000,512]{1,0:T(8,128)(2,1)} %all-gather.4.cloned.1.call-done) | copy-start | bytes 9216004
Sparse Core Ops, SparseCore 0:
  8.9 31.1 all-gather.3
  41.7 213.3 all-gather.5
  257.6 415.1 all-reduce.1
